TPU v7x, 32 devices: a whole 2x2x4 slice. The times are simulated.
32 devices in a mesh: groups: 2 (over y), gx: 4 (over z), gy: 4 (over x, core).
Axes of the slice: x: 2, y: 2, z: 4, core: 2. Of those that a mesh axis runs over, the one named last changes fastest.
Arguments:
- tokens: bfloat16 [2, 16, 16384], P(None, 'groups', 'gx'), parts along dimension 1, may hold values from -20 to 20, as said below
- lengths: int32 [2, 16], P(None, ('groups', 'gx')), parts along dimension 1, may hold values from 1 to 1024, as said below
- norm_gain: bfloat16 [16384], P('gx'), may hold values from 0.5 to 2
- w_query: bfloat16 [16384, 8192], P('gx', 'gy'), may hold values from -1.171875 to 1.171875
- key_value_weight: bfloat16 [16384, 4, 256], P('gx', 'gy'), may hold values from -0.046875 to 0.046875
- w_out: bfloat16 [8192, 16384], P('gy', 'gx'), may hold values from -0.0625 to 0.0625
- cache: bfloat16 [2, 16, 1024, 4, 2, 128], P(None, ('groups', 'gx'), None, 'gy'), parts along dimension 1, may hold values from -16 to 16
Outputs:
- layer_out: bfloat16 [2, 16, 16384], P(None, 'groups', 'gx'), parts along dimension 1
There are 2 independent parts, one for each index of `groups`. A program takes and returns all parts, laid end to end along the dimension named above; an argument that names none is the same for every part. Nothing has to cross between parts.
Inputs may be any that keep to these rules, and one draw needn't show every extreme that they name: `tokens`: entries vary with the feature and the row. `lengths`: some rollout has exactly 1024 cached positions in every draw.
All inputs are finite; a program needn't handle non-finite values.
Results may differ from a plain program's by a relative error of at most 0.012.
The roundings to bfloat16 on the way count: a program that leaves them out, or rounds other values in their place, can miss the bound.
Values may be sent and summed in bfloat16 or wider, within the bound.
No kernel may reach another device: no remote copies, remote signals or barrier semaphores. Data moves between devices by JAX's collectives and lax.ppermute only.
A program may use at most 128 MiB of HBM per device.

v0:
```python
import jax
import jax.numpy as jnp
from jax import lax
from jax.sharding import PartitionSpec as P

MODEL_WIDTH = 16384
HEAD_SIZE = 128


def rotate(vectors, positions):
    half = vectors.shape[-1] // 2
    freq = 500000.0 ** (-2.0 * jnp.arange(half, dtype=jnp.float32) / vectors.shape[-1])
    angle = positions[..., None] * freq
    cosine = jnp.cos(angle)
    sine = jnp.sin(angle)
    first = vectors[..., :half]
    second = vectors[..., half:]
    return jnp.concatenate(
        [first * cosine - second * sine, second * cosine + first * sine], axis=-1
    )


def attend(query_sum, keyval_sum, local_squares, lengths, cache):
    batches, rows_here = lengths.shape
    score_scale = lax.rsqrt(local_squares / MODEL_WIDTH + 1e-05)
    heads_kv = keyval_sum.shape[2]
    query_group = query_sum.shape[2] // (heads_kv * HEAD_SIZE)
    query = (
        query_sum.reshape(batches, rows_here, heads_kv, query_group, HEAD_SIZE)
        * score_scale[:, :, None, None, None]
    )
    key_value = keyval_sum * score_scale[:, :, None, None]
    positions = lengths.astype(jnp.float32)
    rotated_query = rotate(query, positions[:, :, None, None]).astype(jnp.bfloat16)
    rkey = rotate(key_value[..., :HEAD_SIZE], positions[:, :, None])
    value_new = key_value[..., HEAD_SIZE:]
    inv_root = 1.0 / jnp.sqrt(jnp.float32(HEAD_SIZE))
    keys = cache[:, :, :, :, 0, :]
    values = cache[:, :, :, :, 1, :]
    scores = (
        jnp.einsum("mrkgd,mrskd->mrkgs", rotated_query, keys, preferred_element_type=jnp.float32)
        * inv_root
    )
    valid = jnp.arange(cache.shape[2], dtype=jnp.int32)[None, None, :] < lengths[:, :, None]
    scores = jnp.where(valid[:, :, None, None, :], scores, -1e30)
    new_score = (
        jnp.sum(rotated_query.astype(jnp.float32) * rkey[:, :, :, None, :], axis=-1) * inv_root
    )
    top = jnp.maximum(jnp.max(scores, axis=-1), new_score)
    weights = jnp.exp(scores - top[..., None])
    new_weight = jnp.exp(new_score - top)
    total = jnp.sum(weights, axis=-1) + new_weight
    summed = jnp.einsum(
        "mrkgs,mrskd->mrkgd",
        weights.astype(jnp.bfloat16),
        values,
        preferred_element_type=jnp.float32,
    )
    summed = summed + new_weight[..., None] * value_new[:, :, :, None, :]
    return (
        (summed / total[..., None])
        .astype(jnp.bfloat16)
        .reshape(batches, rows_here, heads_kv * query_group * HEAD_SIZE)
    )


def local(tokens, lengths, norm_gain, w_query, key_value_weight, w_out, cache):
    x_full = tokens.astype(jnp.float32)
    squares = jnp.sum(x_full * x_full, axis=-1)
    normed = (x_full * norm_gain.astype(jnp.float32)).astype(jnp.bfloat16)
    query_part = jnp.einsum("mrd,dc->mrc", normed, w_query, preferred_element_type=jnp.float32)
    keyval_part = jnp.einsum(
        "mrd,dkc->mrkc", normed, key_value_weight, preferred_element_type=jnp.float32
    )
    query_sum, keyval_sum, local_squares = (
        lax.psum_scatter(query_part, "gx", scatter_dimension=1, tiled=True),
        lax.psum_scatter(keyval_part, "gx", scatter_dimension=1, tiled=True),
        lax.psum_scatter(squares, "gx", scatter_dimension=1, tiled=True),
    )
    attended = attend(query_sum, keyval_sum, local_squares, lengths, cache)
    projected = jnp.einsum(
        "mrc,cd->mrd",
        lax.all_gather(attended, "gx", axis=1, tiled=True),
        w_out,
        preferred_element_type=jnp.float32,
    )
    summed_heads = lax.psum(projected, "gy")
    return (x_full + summed_heads).astype(jnp.bfloat16)


def solution(mesh):
    placed = (
        P(None, "groups", "gx"),
        P(None, ("groups", "gx")),
        P("gx"),
        P("gx", "gy"),
        P("gx", "gy", None),
        P("gy", "gx"),
        P(None, ("groups", "gx"), None, "gy", None, None),
    )
    return jax.shard_map(
        local, mesh=mesh, in_specs=placed, out_specs=P(None, "groups", "gx"), check_vma=False
    )
```

profile of v0, /device:TPU:0, one launch (start us, length us, event | category | flops | bytes accessed | tf_op | source)
XLA Modules:
  0.0 122.0 jit_solution(11372717634072038642)
XLA Ops:
  6.5 0.8 convert_element_type.46
  7.4 8.8 %fusion.2 = f32[2,8,2048]{2,1,0:T(8,128)} fusion(bf16[4096,2048]{1,0:T(8,128)(2,1)} %param.10, bf16[2,8,4096]{2,1,0:T(8,128)(2,1)} %param.7, f32[4096]{0:T(1024)S(1)} %convert_element_type.46), kind=kOutput, calls=%fused_computation.2 | convolution fusion | flops 268632064 | bytes 17055744 | tf_op jit(solution)/shard_map/mrd,dc->mrc/dot_general | solution.py:71
  16.3 0.1 fusion.13
  16.4 0.1 iota_compare_fusion
  16.5 0.4 fusion.9
  16.9 0.7 dynamic-slice
  18.3 0.1 multiply_cosine_fusion.1
  18.4 20.8 %all-reduce.3 = (f32[2,8]{1,0:T(2,128)S(1)}, f32[2,8,1,256]{3,1,0,2:T(8,128)S(1)}) all-reduce(f32[2,8]{1,0:T(2,128)S(1)} %fusion.13, f32[2,8,1,256]{3,1,0,2:T(8,128)S(1)} %fusion.9), channel_id=3, replica_groups=mesh['groups'=2,'gx'=4,'gy'=4] {'gx'}, use_global_device_ids=true, to_apply=%region_2.0.clone | all-reduce | flops 4112 | bytes 32896
  39.2 0.1 fusion.32
  39.3 0.1 dynamic-slice_multiply_fusion
  39.4 0.1 fusion.29
  39.5 6.9 %fusion.35 = (bf16[2,2,1024,1,1,128]{5,4,3,2,1,0:T(2,128)(2,1)}, bf16[2,2,1024,1,1,128]{5,4,3,2,1,0:T(2,128)(2,1)}) fusion(bf16[2,2,1024,1,2,128]{5,4,3,2,1,0:T(2,128)(2,1)} %param.13), kind=kLoop, calls=%fused_computation.55 | loop fusion | bytes 4194304 | tf_op jit(solution)/shard_map/slice | solution.py:38
  46.4 0.1 maximum_bitcast_fusion
  46.5 7.3 %all-reduce.9.cloned.1.call-done = f32[2,8,2048]{2,1,0:T(8,128)} async-done(((f32[2,8,2048]{2,1,0:T(8,128)}), f32[2,8,2048]{2,1,0:T(8,128)}) %all-reduce.9.cloned.1.call-update) | async-done | bytes 131088
  53.9 0.9 constant_dynamic-slice_fusion
  54.9 0.1 subtract_convert_fusion
  55.0 0.2 multiply_reduce_fusion
  55.1 2.1 %fusion.36 = (f32[2,2,16]{2,1,0:T(2,128)S(1)}, f32[2,2,16,1024]{3,2,1,0:T(8,128)S(1)}) fusion(bf16[2,2,1024,1,1,128]{5,4,3,2,1,0:T(2,128)(2,1)} %get-tuple-element.9, bf16[2,2,16,64]{3,2,1,0:T(8,128)(2,1)S(1)} %bitcast.38, bf16[2,2,16,64]{3,2,1,0:T(8,128)(2,1)S(1)} %bitcast.37, pred[2,2,1024]{2,1,0:T(4,128)(4,1)S(1)} %iota_compare_fusion), kind=kOutput, calls=%fused_computation.56 | convolution fusion | flops 17006528 | bytes 1331456 | tf_op jit(solution)/shard_map/mrkgd,mrskd->mrkgs/dot_general | solution.py:41
  57.3 0.2 fusion.15
  57.5 1.9 %fusion.8 = bf16[2,2,16,128]{3,2,1,0:T(8,128)(2,1)S(1)} fusion(bf16[2,2,1024,1,1,128]{5,4,3,2,1,0:T(2,128)(2,1)} %get-tuple-element.10, f32[2,2,16,1024]{3,2,1,0:T(8,128)S(1)} %get-tuple-element.18, f32[2,2,16]{2,1,0:T(2,128)S(1)} %multiply_maximum_fusion, f32[2,2,16]{2,1,0:T(2,128)S(1)} %get-tuple-element.7, f32[2,2,128]{2,1,0:T(2,128)S(1)} %slice_bitcast_fusion, ...), kind=kOutput, calls=%fused_computation.10 | convolution fusion | flops 16941056 | bytes 1329920 | tf_op jit(solution)/shard_map/mrkgs,mrskd->mrkgd/dot_general | solution.py:53
  59.4 13.1 %all_gather.3 = bf16[2,8,2048]{2,0,1:T(2,128)(2,1)S(1)} all-gather(bf16[2,2,2048]{2,0,1:T(2,128)(2,1)S(1)} %copy.12), channel_id=1, replica_groups=mesh['groups'=2,'gx'=4,'gy'=4] {'gx'}, dimensions={1}, use_global_device_ids=true | all-gather | bytes 81920 | tf_op jit(solution)/shard_map/all_gather | solution.py:83
  72.6 8.8 %fusion = f32[2,8,4096]{2,1,0:T(8,128)} fusion(bf16[2048,4096]{1,0:T(8,128)(2,1)} %param.12, bf16[2,8,2048]{2,0,1:T(2,128)(2,1)S(1)} %all_gather.3), kind=kOutput, calls=%fused_computation | convolution fusion | flops 268435456 | bytes 17104896 | tf_op jit(solution)/shard_map/mrc,cd->mrd/dot_general | solution.py:81
  81.3 32.2 %all-reduce.7.cloned.1.call-done = f32[2,8,4096]{2,1,0:T(8,128)} async-done(((f32[2,8,4096]{2,1,0:T(8,128)}), f32[2,8,4096]{2,1,0:T(8,128)}) %all-reduce.7.cloned.1.call-update) | async-done | bytes 262160 | tf_op jit(solution)/shard_map/psum | solution.py:87
  113.5 1.6 %fusion.14 = bf16[2,8,4096]{2,1,0:T(8,128)(2,1)} fusion(f32[2,8,4096]{2,1,0:T(8,128)} %all-reduce.7.cloned.1.call-done, bf16[2,8,4096]{2,1,0:T(8,128)(2,1)S(1)} %copy-done.1), kind=kLoop, calls=%fused_computation.19 | loop fusion | flops 196608 | bytes 524288 | tf_op jit(solution)/shard_map/convert_element_type | solution.py:88
  (21 shorter events, 0.3 us)
Async XLA Ops:
  6.5 10.0 %copy-start = (bf16[4096,1,256]{2,0,1:T(8,128)(2,1)S(1)}, bf16[4096,1,256]{2,0,1:T(8,128)(2,1)}, u32[]{:S(2)}) copy-start(bf16[4096,1,256]{2,0,1:T(8,128)(2,1)} %param.11) | copy-start | bytes 6291460
  6.5 47.3 %all-reduce.9.cloned.1.call-start = ((), (), s32[]{:S(2)}) async-start(), calls=%async_computation.1 | async-start | bytes 262144
  7.4 8.9 %copy-start.1 = (bf16[2,8,4096]{2,1,0:T(8,128)(2,1)S(1)}, bf16[2,8,4096]{2,1,0:T(8,128)(2,1)}, u32[]{:S(2)}) copy-start(bf16[2,8,4096]{2,1,0:T(8,128)(2,1)} %param.7) | copy-start | bytes 393220
  7.4 9.0 %copy-start.2 = (s32[2,2]{1,0:T(2,128)S(1)}, s32[2,2]{1,0:T(2,128)}, u32[]{:S(2)}) copy-start(s32[2,2]{1,0:T(2,128)} %param.8) | copy-start | bytes 52
  16.2 0.7 copy-start.3
  16.2 97.3 %all-reduce.7.cloned.1.call-start = ((), (), s32[]{:S(2)}) async-start(), calls=%async_computation | async-start | bytes 524288 | tf_op jit(solution)/shard_map/psum | solution.py:87
Sparse Core Ops, SparseCore 0:
  16.4 37.4 all-reduce.8
  81.5 31.9 all-reduce.6
where the time goes:
time: 122 us
  waiting for transfers between devices  39.5 us (32%)
  blocking collectives  33.9 us (28%)
  matrix products  22 us (18%)
  between operations  14.2 us (12%)
  local copies, waits for them, and re-layouts  8.61 us (7%)
  other arithmetic  3.71 us (3%)
    psum x1, waiting for transfers between devices, local(): summed_heads = lax.psum(projected, 'gy')  32.2 us
    unnamed x1, blocking collectives  20.8 us
    all_gather x1, blocking collectives, local(): lax.all_gather(attended, 'gx', axis=1, tiled=True)  13.1 us
    dot_general x1, matrix products, local(): jnp.einsum('mrd,dc->mrc', normed, w_query, preferred_element_type=jnp.flo...  8.81 us
    dot_general x1, matrix products, local(): jnp.einsum('mrc,cd->mrd', lax.all_gather(attended, 'gx', axis=1, tiled=Tr...  8.75 us
    unnamed x3, waiting for transfers between devices  7.38 us
    slice x1, local copies, waits for them, and re-layouts, attend(): keys = cache[:, :, :, :, 0, :]  6.95 us
  transfers between devices with their start and end apart: 2, of which 2 were waited for; matrix products, arithmetic and copies ran while one was open for 7% of the time, Pallas kernels for 0%

commit v1 on v0

--- a/solution.py
+++ b/solution.py
@@ -84,7 +84,11 @@
         w_out,
         preferred_element_type=jnp.float32,
     )
-    summed_heads = lax.psum(projected, "gy")
+    summed_heads = projected
+    for hop in (1, 2):
+        summed_heads = summed_heads + lax.ppermute(
+            summed_heads, "gy", [(dev, dev ^ hop) for dev in range(4)]
+        )
     return (x_full + summed_heads).astype(jnp.bfloat16)
 
 

time: 122 us -> 98.6 us (0.81)
  waiting for transfers between devices: 39.5 us -> 15.9 us
  starting transfers between devices: 0.04 us -> 1.52 us
    psum x1 -> x0, waiting for transfers between devices: 32.2 us -> none  [local(): summed_heads = lax.psum(projected, 'gy')]
    ppermute x0 -> x2, waiting for transfers between devices: none -> 8.44 us  [local(): lax.ppermute(summed_heads, 'gy', [(dev, dev ^ hop) for dev in range(4)])]
    ppermute x0 -> x2, starting transfers between devices: none -> 1.52 us  [local(): lax.ppermute(summed_heads, 'gy', [(dev, dev ^ hop) for dev in range(4)])]
    unnamed x3 -> x2, waiting for transfers between devices: 7.38 us -> 7.49 us
  transfers between devices with their start and end apart: 2 -> 3, of which waited for: 2 -> 3; matrix products, arithmetic and copies ran while one was open for 7% -> 9% of each run, Pallas kernels for 0% -> 0%
where the time goes in v1:
time: 98.6 us; the launch traced here: 98.2 us
  blocking collectives  33.9 us (34%)
  matrix products  21.2 us (22%)
  waiting for transfers between devices  15.9 us (16%)
  between operations  14.2 us (14%)
  local copies, waits for them, and re-layouts  8.62 us (9%)
  other arithmetic  2.81 us (3%)
  starting transfers between devices  1.52 us (2%)
    unnamed x1, blocking collectives  20.8 us
    all_gather x1, blocking collectives, local(): lax.all_gather(attended, 'gx', axis=1, tiled=True)  13.1 us
    dot_general x1, matrix products, local(): jnp.einsum('mrd,dc->mrc', normed, w_query, preferred_element_type=jnp.flo...  8.81 us
    ppermute x2, waiting for transfers between devices, local(): lax.ppermute(summed_heads, 'gy', [(dev, dev ^ hop) for dev in range(4)])  8.44 us
    dot_general x1, matrix products, local(): jnp.einsum('mrc,cd->mrd', lax.all_gather(attended, 'gx', axis=1, tiled=Tr...  8.05 us
    unnamed x2, waiting for transfers between devices  7.49 us
    slice x1, local copies, waits for them, and re-layouts, attend(): keys = cache[:, :, :, :, 0, :]  6.95 us
    dot_general x1, matrix products, attend(): jnp.einsum('mrkgd,mrskd->mrkgs', rotated_query, keys, preferred_element_t...  2.1 us
  transfers between devices with their start and end apart: 3, of which 3 were waited for; matrix products, arithmetic and copies ran while one was open for 9% of the time, Pallas kernels for 0%

profile of v1, /device:TPU:0, one launch (start us, length us, event | category | flops | bytes accessed | tf_op | source)
XLA Modules:
  0.0 98.2 jit_solution(3307782136391709353)
XLA Ops:
  6.5 0.8 convert_element_type.46
  7.4 8.8 %fusion.2 = f32[2,8,2048]{2,1,0:T(8,128)} fusion(bf16[4096,2048]{1,0:T(8,128)(2,1)} %param.10, bf16[2,8,4096]{2,1,0:T(8,128)(2,1)} %param.7, f32[4096]{0:T(1024)S(1)} %convert_element_type.46), kind=kOutput, calls=%fused_computation.2 | convolution fusion | flops 268632064 | bytes 17055744 | tf_op jit(solution)/shard_map/mrd,dc->mrc/dot_general | solution.py:71
  16.3 0.1 fusion.13
  16.4 0.1 iota_compare_fusion
  16.5 0.4 fusion.9
  16.9 0.7 dynamic-slice
  18.2 0.1 multiply_cosine_fusion.1
  18.4 20.8 %all-reduce.3 = (f32[2,8]{1,0:T(2,128)S(1)}, f32[2,8,1,256]{3,1,0,2:T(8,128)S(1)}) all-reduce(f32[2,8]{1,0:T(2,128)S(1)} %fusion.13, f32[2,8,1,256]{3,1,0,2:T(8,128)S(1)} %fusion.9), channel_id=3, replica_groups=mesh['groups'=2,'gx'=4,'gy'=4] {'gx'}, use_global_device_ids=true, to_apply=%region_2.0.clone | all-reduce | flops 4112 | bytes 32896
  39.2 0.1 dynamic-slice_multiply_fusion
  39.3 0.1 fusion.29
  39.4 7.0 %fusion.35 = (bf16[2,2,1024,1,1,128]{5,4,3,2,1,0:T(2,128)(2,1)}, bf16[2,2,1024,1,1,128]{5,4,3,2,1,0:T(2,128)(2,1)}) fusion(bf16[2,2,1024,1,2,128]{5,4,3,2,1,0:T(2,128)(2,1)} %param.13), kind=kLoop, calls=%fused_computation.55 | loop fusion | bytes 4194304 | tf_op jit(solution)/shard_map/slice | solution.py:38
  46.4 7.5 %all-reduce.6.cloned.1.call-done = f32[2,8,2048]{2,1,0:T(8,128)} async-done(((f32[2,8,2048]{2,1,0:T(8,128)}), f32[2,8,2048]{2,1,0:T(8,128)}) %all-reduce.6.cloned.1.call-update) | async-done | bytes 131088
  53.9 0.9 constant_dynamic-slice_fusion
  54.9 0.1 subtract_convert_fusion
  55.0 0.2 multiply_reduce_fusion
  55.2 2.1 %fusion.36 = (f32[2,2,16]{2,1,0:T(2,128)S(1)}, f32[2,2,16,1024]{3,2,1,0:T(8,128)S(1)}) fusion(bf16[2,2,1024,1,1,128]{5,4,3,2,1,0:T(2,128)(2,1)} %get-tuple-element.9, bf16[2,2,16,64]{3,2,1,0:T(8,128)(2,1)S(1)} %bitcast.38, bf16[2,2,16,64]{3,2,1,0:T(8,128)(2,1)S(1)} %bitcast.37, pred[2,2,1024]{2,1,0:T(4,128)(4,1)S(1)} %iota_compare_fusion), kind=kOutput, calls=%fused_computation.56 | convolution fusion | flops 17006528 | bytes 1331456 | tf_op jit(solution)/shard_map/mrkgd,mrskd->mrkgs/dot_general | solution.py:41
  57.3 0.2 fusion.15
  57.5 1.9 %fusion.8 = bf16[2,2,16,128]{3,2,1,0:T(8,128)(2,1)S(1)} fusion(bf16[2,2,1024,1,1,128]{5,4,3,2,1,0:T(2,128)(2,1)} %get-tuple-element.10, f32[2,2,16,1024]{3,2,1,0:T(8,128)S(1)} %get-tuple-element.18, f32[2,2,16]{2,1,0:T(2,128)S(1)} %multiply_maximum_fusion, f32[2,2,16]{2,1,0:T(2,128)S(1)} %get-tuple-element.7, f32[2,2,128]{2,1,0:T(2,128)S(1)} %slice_bitcast_fusion, ...), kind=kOutput, calls=%fused_computation.10 | convolution fusion | flops 16941056 | bytes 1329920 | tf_op jit(solution)/shard_map/mrkgs,mrskd->mrkgd/dot_general | solution.py:53
  59.5 13.1 %all_gather.3 = bf16[2,8,2048]{2,0,1:T(2,128)(2,1)S(1)} all-gather(bf16[2,2,2048]{2,0,1:T(2,128)(2,1)S(1)} %copy.12), channel_id=1, replica_groups=mesh['groups'=2,'gx'=4,'gy'=4] {'gx'}, dimensions={1}, use_global_device_ids=true | all-gather | bytes 81920 | tf_op jit(solution)/shard_map/all_gather | solution.py:83
  72.6 8.0 %fusion = f32[2,8,4096]{2,1,0:T(8,128)S(1)} fusion(bf16[2048,4096]{1,0:T(8,128)(2,1)} %param.12, bf16[2,8,2048]{2,0,1:T(2,128)(2,1)S(1)} %all_gather.3), kind=kOutput, calls=%fused_computation | convolution fusion | flops 268435456 | bytes 17104896 | tf_op jit(solution)/shard_map/mrc,cd->mrd/dot_general | solution.py:81
  80.7 1.5 %collective-permute-done = f32[2,8,4096]{2,1,0:T(8,128)S(1)} collective-permute-done((f32[2,8,4096]{2,1,0:T(8,128)S(1)}, f32[2,8,4096]{2,1,0:T(8,128)S(1)}, u32[]{:S(2)}, u32[]{:S(2)}) %collective-permute-start) | collective-permute-done | bytes 262176 | tf_op jit(solution)/shard_map/ppermute | solution.py:89
  82.2 1.5 %collective-permute-start.1 = (f32[2,8,4096]{2,1,0:T(8,128)S(1)}, f32[2,8,4096]{2,1,0:T(8,128)S(1)}, u32[]{:S(2)}, u32[]{:S(2)}) collective-permute-start(f32[2,8,4096]{2,1,0:T(8,128)S(1)} %add.42), channel_id=1, source_target_pairs={{0,2},{1,3},{2,0},{3,1},{4,6},{5,7},{6,4},{7,5},{8,10},{9,11},{10,... | collective-permute-start | bytes 786440 | tf_op jit(solution)/shard_map/ppermute | solution.py:89
  83.7 6.9 %collective-permute-done.1 = f32[2,8,4096]{2,1,0:T(8,128)S(1)} collective-permute-done((f32[2,8,4096]{2,1,0:T(8,128)S(1)}, f32[2,8,4096]{2,1,0:T(8,128)S(1)}, u32[]{:S(2)}, u32[]{:S(2)}) %collective-permute-start.1) | collective-permute-done | bytes 262176 | tf_op jit(solution)/shard_map/ppermute | solution.py:89
  90.6 0.7 fusion.14
  (23 shorter events, 0.4 us)
Async XLA Ops:
  6.5 9.9 %copy-start = (bf16[4096,1,256]{2,0,1:T(8,128)(2,1)S(1)}, bf16[4096,1,256]{2,0,1:T(8,128)(2,1)}, u32[]{:S(2)}) copy-start(bf16[4096,1,256]{2,0,1:T(8,128)(2,1)} %param.11) | copy-start | bytes 6291460
  6.5 47.4 %all-reduce.6.cloned.1.call-start = ((), (), s32[]{:S(2)}) async-start(), calls=%async_computation | async-start | bytes 262144
  7.4 8.9 %copy-start.1 = (bf16[2,8,4096]{2,1,0:T(8,128)(2,1)S(1)}, bf16[2,8,4096]{2,1,0:T(8,128)(2,1)}, u32[]{:S(2)}) copy-start(bf16[2,8,4096]{2,1,0:T(8,128)(2,1)} %param.7) | copy-start | bytes 393220
  7.4 9.0 %copy-start.2 = (s32[2,2]{1,0:T(2,128)S(1)}, s32[2,2]{1,0:T(2,128)}, u32[]{:S(2)}) copy-start(s32[2,2]{1,0:T(2,128)} %param.8) | copy-start | bytes 52
  16.2 0.7 copy-start.3
  80.7 1.5 %collective-permute-start = (f32[2,8,4096]{2,1,0:T(8,128)S(1)}, f32[2,8,4096]{2,1,0:T(8,128)S(1)}, u32[]{:S(2)}, u32[]{:S(2)}) collective-permute-start(f32[2,8,4096]{2,1,0:T(8,128)S(1)} %fusion), channel_id=1, source_target_pairs={{0,1},{1,0},{2,3},{3,2},{4,5},{5,4},{6,7},{7,6},{8,9},{9,8},{10,11... | collective-permute-start | bytes 786440 | tf_op jit(solution)/shard_map/ppermute | solution.py:89
  82.2 8.4 %collective-permute-start.1 = (f32[2,8,4096]{2,1,0:T(8,128)S(1)}, f32[2,8,4096]{2,1,0:T(8,128)S(1)}, u32[]{:S(2)}, u32[]{:S(2)}) collective-permute-start(f32[2,8,4096]{2,1,0:T(8,128)S(1)} %add.42), channel_id=1, source_target_pairs={{0,2},{1,3},{2,0},{3,1},{4,6},{5,7},{6,4},{7,5},{8,10},{9,11},{10,... | collective-permute-start | bytes 786440 | tf_op jit(solution)/shard_map/ppermute | solution.py:89
Sparse Core Ops, SparseCore 0:
  16.4 37.5 all-reduce.5
